TPU v7x, 32 devices: a whole 2x2x4 slice. The times are simulated.
32 devices in a mesh: row: 8 (over y, x, core), col: 4 (over z).
Axes of the slice: x: 2, y: 2, z: 4, core: 2. Of those that a mesh axis runs over, the one named last changes fastest.
Arguments:
- vectors: bfloat16 [32, 1024, 512], P('col', 'row'), may hold values from -6 to 6
- right_factors: bfloat16 [32, 32, 1024, 128], P('row', 'col'), may hold values from -0.1875 to 0.1875
- left_factors: bfloat16 [32, 32, 1024, 128], P('row', 'col'), may hold values from -0.125 to 0.125
- tile_ranks: int32 [32, 32], P('row', 'col'), may hold values from 16 to 128
- owner_map: int32 [32], replicated, may hold values from 0 to 31, as said below
Outputs:
- applied: bfloat16 [32, 1024, 512], P('row', 'col')
Inputs may be any that keep to these rules, and one draw needn't show every extreme that they name: owner_map is a permutation of 0 to 31; the 4 stored tile rows held by index i of row (stored rows i * 4 to i * 4 + 3) belong to 4 different indices of row of applied, i + c mod 8 for the same 4 offsets c at every i.
All inputs are finite; a program needn't handle non-finite values.
Results may differ from a plain program's by a relative error of at most 0.0066.
Values may be sent and summed in bfloat16 or wider, within the bound.
A program may use at most 128 MiB of HBM per device.

v0:
```python
import jax
import jax.numpy as jnp
from jax import lax
from jax.sharding import PartitionSpec as P


def masked_coeffs(products, tile_ranks, rank_width):
    columns = jnp.arange(rank_width, dtype=jnp.int32)
    kept_mask = columns[None, None, :] < tile_ranks[:, :, None]
    return jnp.where(kept_mask[:, :, :, None], products, 0.0).astype(jnp.bfloat16)


def build_buffer(payload, owner_map, cycle_size):
    held_rows = payload.shape[0]
    own_rows = lax.dynamic_slice_in_dim(owner_map, lax.axis_index("row") * held_rows, held_rows)
    target = own_rows // held_rows
    devices = jnp.arange(cycle_size, dtype=jnp.int32)
    matches = target[None, :] == devices[:, None]
    present = jnp.any(matches, axis=1)
    source_slot = jnp.sum(
        jnp.where(matches, jnp.arange(held_rows, dtype=jnp.int32)[None, :], 0), axis=1
    )
    picked = jnp.take(payload, source_slot, axis=0)
    return jnp.where(present[:, None, None], picked, jnp.zeros_like(picked))


def pick_rows(received, owner_map, held_rows):
    wanted = lax.axis_index("row") * held_rows + jnp.arange(held_rows, dtype=jnp.int32)
    matches = owner_map[None, :] == wanted[:, None]
    anchor = jnp.sum(
        jnp.where(matches, jnp.arange(owner_map.shape[0], dtype=jnp.int32)[None, :], 0), axis=1
    )
    return jnp.take(received, anchor // held_rows, axis=0)


def on_device(vectors, right_factors, left_factors, tile_ranks, owner_map):
    held_rows = right_factors.shape[0]
    rank_width = right_factors.shape[3]
    cycle_size = lax.axis_size("row")
    products = jnp.einsum(
        "ikbr,kbv->ikrv",
        right_factors,
        lax.all_gather(vectors, "row", axis=1, tiled=True),
        preferred_element_type=jnp.float32,
    )
    coeffs = masked_coeffs(products, tile_ranks, rank_width)
    partial_rows = jnp.einsum(
        "ikbr,ikrv->ibv", left_factors, coeffs, preferred_element_type=jnp.float32
    )
    summed = lax.psum_scatter(partial_rows, "col", scatter_dimension=1, tiled=True).astype(
        jnp.bfloat16
    )
    buffer = build_buffer(summed, owner_map, cycle_size)
    received = lax.all_to_all(buffer, "row", split_axis=0, concat_axis=0, tiled=True)
    applied = pick_rows(received, owner_map, held_rows)
    return applied


def solution(mesh):
    placed = (
        P("col", "row", None),
        P("row", "col", None, None),
        P("row", "col", None, None),
        P("row", "col"),
        P(),
    )
    return jax.shard_map(
        on_device, mesh=mesh, in_specs=placed, out_specs=P("row", "col", None), check_vma=False
    )
```

profile of v0, /device:TPU:0, one launch (start us, length us, event | category | flops | bytes accessed | tf_op | source)
XLA Modules:
  0.0 271.4 jit_solution(948302696471374495)
XLA Ops:
  6.5 0.0 all-gather.2.cloned.1.call-start
  6.5 0.7 all-gather.2.cloned.1.call-update
  7.3 0.0 reduce-scatter.2.cloned.1.call-start
  7.3 0.8 iota_compare_fusion
  8.1 58.2 %all-gather.2.cloned.1.call-done = bf16[8,1024,512]{2,1,0:T(8,128)(2,1)} async-done(((bf16[8,128,512]{2,1,0:T(8,128)(2,1)}), bf16[8,1024,512]{2,1,0:T(8,128)(2,1)}) %all-gather.2.cloned.1.call-update) | async-done | bytes 8388624 | tf_op jit(solution)/shard_map/all_gather | solution.py:43
  66.3 17.0 %fusion.7 = f32[4,1024,512]{1,2,0:T(8,128)} fusion(bf16[4,8,1024,128]{3,2,1,0:T(8,128)(2,1)} %param.7, pred[4,8,128]{2,1,0:T(8,128)(4,1)S(1)} %iota_compare_fusion, bf16[4,8,1024,128]{3,2,1,0:T(8,128)(2,1)} %param.6, bf16[8,1024,512]{2,1,0:T(8,128)(2,1)} %all-gather.2.cloned.1.call-done), kind=kOutput, calls=%fused_computation.9 | convolution fusion | flops 8594128896 | bytes 33558528 | tf_op jit(solution)/shard_map/ikbr,ikrv->ibv/dot_general | solution.py:47
  83.3 0.0 copy-start
  83.3 0.0 reduce-scatter.2.cloned.1.call-update
  83.3 0.6 copy-done
  83.9 0.1 and_select_fusion.1
  84.0 0.1 select_reduce_fusion
  84.1 0.1 fusion.14
  84.2 143.9 %reduce-scatter.2.cloned.1.call-done = f32[4,256,512]{1,2,0:T(8,128)} async-done(((f32[4,1024,512]{1,2,0:T(8,128)}), f32[4,256,512]{1,2,0:T(8,128)}) %reduce-scatter.2.cloned.1.call-update) | async-done | bytes 2097168 | tf_op jit(solution)/shard_map/reduce_scatter | solution.py:50
  228.1 1.7 convert_element_type.7
  229.8 0.7 gather_fusion
  230.5 1.6 select_select_fusion
  232.1 3.7 %all-to-all-start = ((bf16[8,256,512]{1,2,0:T(8,128)(2,1)}), bf16[8,256,512]{1,2,0:T(8,128)(2,1)S(1)}, u32[]{:S(2)}, u32[]{:S(2)}) async-start(bf16[8,256,512]{1,2,0:T(8,128)(2,1)} %select_select_fusion), calls=%async_computation.1 | async-start | bytes 4194304 | tf_op jit(solution)/shard_map/all_to_all | solution.py:54
  235.8 0.2 select_reduce_fusion.1
  236.0 26.4 %all-to-all-done = bf16[8,256,512]{1,2,0:T(8,128)(2,1)S(1)} async-done(((bf16[8,256,512]{1,2,0:T(8,128)(2,1)}), bf16[8,256,512]{1,2,0:T(8,128)(2,1)S(1)}, u32[]{:S(2)}, u32[]{:S(2)}) %all-to-all-start) | async-done | bytes 2097184 | tf_op jit(solution)/shard_map/all_to_all | solution.py:54
  262.4 0.6 gather_fusion.1
  263.0 0.2 broadcast_select_fusion
  263.2 1.3 copy.7
  (7 shorter events, 0.1 us)
Async XLA Ops:
  6.5 59.7 %all-gather.2.cloned.1.call-start = ((), (), s32[]{:S(2)}) async-start(), calls=%async_computation.2 | async-start | bytes 9437184 | tf_op jit(solution)/shard_map/all_gather | solution.py:43
  7.3 220.8 %reduce-scatter.2.cloned.1.call-start = ((), (), s32[]{:S(2)}) async-start(), calls=%async_computation.3 | async-start | bytes 10485760 | tf_op jit(solution)/shard_map/reduce_scatter | solution.py:50
  83.3 0.7 copy-start
  232.1 30.3 %all-to-all-start = ((bf16[8,256,512]{1,2,0:T(8,128)(2,1)}), bf16[8,256,512]{1,2,0:T(8,128)(2,1)S(1)}, u32[]{:S(2)}, u32[]{:S(2)}) async-start(bf16[8,256,512]{1,2,0:T(8,128)(2,1)} %select_select_fusion), calls=%async_computation.1 | async-start | bytes 4194304 | tf_op jit(solution)/shard_map/all_to_all | solution.py:54
Sparse Core Ops, SparseCore 0:
  9.2 56.9 all-gather.1
  83.4 144.6 reduce-scatter.1
where the time goes:
time: 272 us; the launch traced here: 271 us
  waiting for transfers between devices  229 us (84%)
  matrix products  17 us (6%)
  between operations  13.4 us (5%)
  other arithmetic  4.76 us (2%)
  starting transfers between devices  3.7 us (1%)
  local copies, waits for them, and re-layouts  3.24 us (1%)
    reduce_scatter x1, waiting for transfers between devices, on_device(): lax.psum_scatter(partial_rows, 'col', scatter_dimension=1, tiled=True)  144 us
    all_gather x1, waiting for transfers between devices, on_device(): lax.all_gather(vectors, 'row', axis=1, tiled=True)  58.2 us
    all_to_all x1, waiting for transfers between devices, on_device(): lax.all_to_all(buffer, 'row', split_axis=0, concat_axis=0, tiled=True)  26.4 us
    dot_general x1, matrix products, on_device(): jnp.einsum('ikbr,ikrv->ibv', left_factors, coeffs, preferred_element_type...  17 us
  transfers between devices with their start and end apart: 3, of which 3 were waited for; matrix products, arithmetic and copies ran while one was open for 0% of the time, Pallas kernels for 0%

commit v1 on v0

--- a/solution.py
+++ b/solution.py
@@ -37,12 +37,38 @@
     held_rows = right_factors.shape[0]
     rank_width = right_factors.shape[3]
     cycle_size = lax.axis_size("row")
-    products = jnp.einsum(
+    length, index, rows = (lax.axis_size("row"), lax.axis_index("row"), vectors.shape[1])
+    ahead = [(i, (i + 1) % length) for i in range(length)]
+    downward = [(i, (i - 1) % length) for i in range(length)]
+    half = length // 2
+    from_left = from_right = vectors
+    total = jnp.einsum(
         "ikbr,kbv->ikrv",
-        right_factors,
-        lax.all_gather(vectors, "row", axis=1, tiled=True),
+        lax.dynamic_slice_in_dim(right_factors, index * rows, vectors.shape[1], axis=2),
+        vectors,
         preferred_element_type=jnp.float32,
     )
+    for lap in range(1, half + 1):
+        from_left = lax.ppermute(from_left, "row", ahead)
+        if lap < length - half:
+            from_right = lax.ppermute(from_right, "row", downward)
+            total = total + jnp.einsum(
+                "ikbr,kbv->ikrv",
+                lax.dynamic_slice_in_dim(
+                    right_factors, (index + lap) % length * rows, from_right.shape[1], axis=2
+                ),
+                from_right,
+                preferred_element_type=jnp.float32,
+            )
+        total = total + jnp.einsum(
+            "ikbr,kbv->ikrv",
+            lax.dynamic_slice_in_dim(
+                right_factors, (index - lap) % length * rows, from_left.shape[1], axis=2
+            ),
+            from_left,
+            preferred_element_type=jnp.float32,
+        )
+    products = total
     coeffs = masked_coeffs(products, tile_ranks, rank_width)
     partial_rows = jnp.einsum(
         "ikbr,ikrv->ibv", left_factors, coeffs, preferred_element_type=jnp.float32

time: 272 us -> 309 us (1.14)
  matrix products: 17 us -> 59.6 us
  waiting for transfers between devices: 229 us -> 213 us
  starting transfers between devices: 3.7 us -> 15 us
    all_gather x1 -> x0, waiting for transfers between devices: 58.2 us -> none  [on_device(): lax.all_gather(vectors, 'row', axis=1, tiled=True)]
    ppermute x0 -> x7, waiting for transfers between devices: none -> 40.1 us  [the longest x4 36.6 us: on_device(): from_left = lax.ppermute(from_left, 'row', ahead)]
    dot_general x0 -> x7, matrix products: none -> 33.2 us  [the longest x6 27 us: on_device(): jnp.einsum('ikbr,kbv->ikrv', lax.dynamic_slice_in_dim(right_factors, (ind...]
    ppermute x0 -> x7, starting transfers between devices: none -> 11.4 us  [the longest x3 7.61 us: on_device(): from_right = lax.ppermute(from_right, 'row', downward)]
    dot_general x1, matrix products: 17 us -> 26.4 us  [on_device(): jnp.einsum('ikbr,ikrv->ibv', left_factors, coeffs, preferred_element_type...]
  transfers between devices with their start and end apart: 3 -> 9, of which waited for: 3 -> 8; matrix products, arithmetic and copies ran while one was open for 0% -> 11% of each run, Pallas kernels for 0% -> 0%
where the time goes in v1:
time: 309 us
  waiting for transfers between devices  213 us (69%)
  matrix products  59.6 us (19%)
  starting transfers between devices  15 us (5%)
  between operations  13.4 us (4%)
  other arithmetic  4.06 us (1%)
  local copies, waits for them, and re-layouts  3.25 us (1%)
    reduce_scatter x1, waiting for transfers between devices, on_device(): lax.psum_scatter(partial_rows, 'col', scatter_dimension=1, tiled=True)  147 us
    ppermute x4, waiting for transfers between devices, on_device(): from_left = lax.ppermute(from_left, 'row', ahead)  36.6 us
    dot_general x6, matrix products, on_device(): jnp.einsum('ikbr,kbv->ikrv', lax.dynamic_slice_in_dim(right_factors, (ind...  27 us
    all_to_all x1, waiting for transfers between devices, on_device(): lax.all_to_all(buffer, 'row', split_axis=0, concat_axis=0, tiled=True)  26.4 us
    dot_general x1, matrix products, on_device(): jnp.einsum('ikbr,ikrv->ibv', left_factors, coeffs, preferred_element_type...  26.4 us
    ppermute x3, starting transfers between devices, on_device(): from_right = lax.ppermute(from_right, 'row', downward)  7.61 us
    dot_general x1, matrix products, on_device(): jnp.einsum('ikbr,kbv->ikrv', lax.dynamic_slice_in_dim(right_factors, inde...  6.21 us
  transfers between devices with their start and end apart: 9, of which 8 were waited for; matrix products, arithmetic and copies ran while one was open for 11% of the time, Pallas kernels for 0%

profile of v1, /device:TPU:0, one launch (start us, length us, event | category | flops | bytes accessed | tf_op | source)
XLA Modules:
  0.0 308.6 jit_solution(6477970531412108000)
XLA Ops:
  6.5 0.5 collective-permute-start.1
  7.0 2.9 collective-permute-start
  9.9 21.3 %collective-permute-done.1 = bf16[8,128,512]{2,1,0:T(8,128)(2,1)S(1)} collective-permute-done((bf16[8,128,512]{2,1,0:T(8,128)(2,1)}, bf16[8,128,512]{2,1,0:T(8,128)(2,1)S(1)}, u32[]{:S(2)}, u32[]{:S(2)}) %collective-permute-start.1) | collective-permute-done | bytes 1048608 | tf_op jit(solution)/shard_map/ppermute | solution.py:52
  31.2 0.7 collective-permute-start.3
  31.9 6.2 %fusion.24 = f32[8,4,128,512]{2,3,0,1:T(8,128)} fusion(bf16[8,128,512]{2,1,0:T(8,128)(2,1)} %param.5, bf16[4,8,1024,128]{3,2,1,0:T(8,128)(2,1)} %param.6, s32[]{:T(128)S(6)} %select_n.139), kind=kOutput, calls=%fused_computation.23 | convolution fusion | flops 536870912 | bytes 10485764 | tf_op jit(solution)/shard_map/ikbr,kbv->ikrv/dot_general | solution.py:45
  38.2 1.9 collective-permute-start.2
  40.2 8.6 %collective-permute-done.3 = bf16[8,128,512]{2,1,0:T(8,128)(2,1)S(1)} collective-permute-done((bf16[8,128,512]{2,1,0:T(8,128)(2,1)S(1)}, bf16[8,128,512]{2,1,0:T(8,128)(2,1)S(1)}, u32[]{:S(2)}, u32[]{:S(2)}) %collective-permute-start.3) | collective-permute-done | bytes 1048608 | tf_op jit(solution)/shard_map/ppermute | solution.py:52
  48.8 2.0 collective-permute-start.5
  50.8 4.5 %fusion.20 = f32[8,4,128,512]{2,3,0,1:T(8,128)} fusion(bf16[8,128,512]{2,1,0:T(8,128)(2,1)S(1)} %collective-permute-done.1, bf16[4,8,1024,128]{3,2,1,0:T(8,128)(2,1)S(1)} %copy-done, s32[]{:T(128)S(6)} %select_n.143), kind=kOutput, calls=%fused_computation.19 | convolution fusion | flops 536870912 | bytes 10485764 | tf_op jit(solution)/shard_map/ikbr,kbv->ikrv/dot_general | solution.py:63
  55.3 4.5 %fusion.22 = f32[8,4,128,512]{2,3,0,1:T(8,128)} fusion(bf16[8,128,512]{2,1,0:T(8,128)(2,1)S(1)} %collective-permute-done, bf16[4,8,1024,128]{3,2,1,0:T(8,128)(2,1)S(1)} %copy-done, s32[]{:T(128)S(6)} %select_n.141), kind=kOutput, calls=%fused_computation.21 | convolution fusion | flops 536870912 | bytes 10485764 | tf_op jit(solution)/shard_map/ikbr,kbv->ikrv/dot_general | solution.py:55
  59.8 0.8 collective-permute-done.2
  60.7 2.8 collective-permute-start.4
  63.5 4.5 %fusion.16 = f32[8,4,128,512]{2,3,0,1:T(8,128)} fusion(bf16[8,128,512]{2,1,0:T(8,128)(2,1)S(1)} %collective-permute-done.3, bf16[4,8,1024,128]{3,2,1,0:T(8,128)(2,1)S(1)} %copy-done, s32[]{:T(128)S(6)} %select_n.147), kind=kOutput, calls=%fused_computation.15 | convolution fusion | flops 536870912 | bytes 10485764 | tf_op jit(solution)/shard_map/ikbr,kbv->ikrv/dot_general | solution.py:63
  68.0 3.9 %collective-permute-done.5 = bf16[8,128,512]{2,1,0:T(8,128)(2,1)S(1)} collective-permute-done((bf16[8,128,512]{2,1,0:T(8,128)(2,1)S(1)}, bf16[8,128,512]{2,1,0:T(8,128)(2,1)S(1)}, u32[]{:S(2)}, u32[]{:S(2)}) %collective-permute-start.5) | collective-permute-done | bytes 1048608 | tf_op jit(solution)/shard_map/ppermute | solution.py:52
  71.9 0.5 collective-permute-start.6
  72.4 4.5 %fusion.18 = f32[8,4,128,512]{2,3,0,1:T(8,128)} fusion(bf16[8,128,512]{2,1,0:T(8,128)(2,1)S(1)} %collective-permute-done.2, bf16[4,8,1024,128]{3,2,1,0:T(8,128)(2,1)S(1)} %copy-done, s32[]{:T(128)S(6)} %select_n.145), kind=kOutput, calls=%fused_computation.17 | convolution fusion | flops 536870912 | bytes 10485764 | tf_op jit(solution)/shard_map/ikbr,kbv->ikrv/dot_general | solution.py:55
  76.9 4.5 %fusion.12 = f32[8,4,128,512]{2,3,0,1:T(8,128)} fusion(bf16[8,128,512]{2,1,0:T(8,128)(2,1)S(1)} %collective-permute-done.5, bf16[4,8,1024,128]{3,2,1,0:T(8,128)(2,1)S(1)} %copy-done, s32[]{:T(128)S(6)} %select_n.151), kind=kOutput, calls=%fused_computation.11 | convolution fusion | flops 536870912 | bytes 10485764 | tf_op jit(solution)/shard_map/ikbr,kbv->ikrv/dot_general | solution.py:63
  81.4 2.6 collective-permute-done.4
  84.0 4.5 %fusion.14 = f32[8,4,128,512]{2,3,0,1:T(8,128)} fusion(bf16[8,128,512]{2,1,0:T(8,128)(2,1)S(1)} %collective-permute-done.4, bf16[4,8,1024,128]{3,2,1,0:T(8,128)(2,1)S(1)} %copy-done, s32[]{:T(128)S(6)} %select_n.149), kind=kOutput, calls=%fused_computation.13 | convolution fusion | flops 536870912 | bytes 10485764 | tf_op jit(solution)/shard_map/ikbr,kbv->ikrv/dot_general | solution.py:55
  88.5 2.8 collective-permute-done.6
  91.3 26.4 %fusion.5 = f32[4,1024,512]{1,2,0:T(8,128)} fusion(bf16[4,8,1024,128]{3,2,1,0:T(8,128)(2,1)} %param.7, f32[8,4,128,512]{2,3,0,1:T(8,128)} %fusion.12, f32[8,4,128,512]{2,3,0,1:T(8,128)} %fusion.14, f32[8,4,128,512]{2,3,0,1:T(8,128)} %fusion.16, f32[8,4,128,512]{2,3,0,1:T(8,128)} %fusion.18, f32[8,4,128,512]{2,3,0,1:T(8,128)} %fusion.20, ...), kind=kOutput, calls=%fused_computation.7 | convolution fusion | flops 4850712576 | bytes 77598720 | tf_op jit(solution)/shard_map/ikbr,ikrv->ibv/dot_general | solution.py:73
  117.7 0.6 copy-done.2
  118.6 146.7 %reduce-scatter.2.cloned.1.call-done = f32[4,256,512]{1,2,0:T(8,128)} async-done(((f32[4,1024,512]{1,2,0:T(8,128)}), f32[4,256,512]{1,2,0:T(8,128)}) %reduce-scatter.2.cloned.1.call-update) | async-done | bytes 2097168 | tf_op jit(solution)/shard_map/reduce_scatter | solution.py:76
  265.4 1.7 convert_element_type.7
  267.0 0.7 gather_fusion
  267.7 1.6 select_select_fusion
  269.4 3.7 %all-to-all-start = ((bf16[8,256,512]{1,2,0:T(8,128)(2,1)}), bf16[8,256,512]{1,2,0:T(8,128)(2,1)S(1)}, u32[]{:S(2)}, u32[]{:S(2)}) async-start(bf16[8,256,512]{1,2,0:T(8,128)(2,1)} %select_select_fusion), calls=%async_computation.1 | async-start | bytes 4194304 | tf_op jit(solution)/shard_map/all_to_all | solution.py:80
  273.0 0.2 select_reduce_fusion.1
  273.3 26.4 %all-to-all-done = bf16[8,256,512]{1,2,0:T(8,128)(2,1)S(1)} async-done(((bf16[8,256,512]{1,2,0:T(8,128)(2,1)}), bf16[8,256,512]{1,2,0:T(8,128)(2,1)S(1)}, u32[]{:S(2)}, u32[]{:S(2)}) %all-to-all-start) | async-done | bytes 2097184 | tf_op jit(solution)/shard_map/all_to_all | solution.py:80
  299.6 0.6 gather_fusion.1
  300.3 0.2 broadcast_select_fusion
  300.4 1.3 copy.7
  (19 shorter events, 0.4 us)
Async XLA Ops:
  6.5 33.6 %copy-start.1 = (s32[4,8]{1,0:T(4,128)S(1)}, s32[4,8]{1,0:T(4,128)}, u32[]{:S(2)}) copy-start(s32[4,8]{1,0:T(4,128)} %param.8) | copy-start | bytes 388
  6.5 258.8 %reduce-scatter.2.cloned.1.call-start = ((), (), s32[]{:S(2)}) async-start(), calls=%async_computation.2 | async-start | bytes 10485760 | tf_op jit(solution)/shard_map/reduce_scatter | solution.py:76
  6.5 24.7 %collective-permute-start.1 = (bf16[8,128,512]{2,1,0:T(8,128)(2,1)}, bf16[8,128,512]{2,1,0:T(8,128)(2,1)S(1)}, u32[]{:S(2)}, u32[]{:S(2)}) collective-permute-start(bf16[8,128,512]{2,1,0:T(8,128)(2,1)} %param.5), channel_id=1, source_target_pairs={{0,4},{4,8},{8,12},{12,16},{16,20},{20,24},{24,28},{28,0},{1,5},{5... | collective-permute-start | bytes 3145736 | tf_op jit(solution)/shard_map/ppermute | solution.py:52
  7.0 31.1 %collective-permute-start = (bf16[8,128,512]{2,1,0:T(8,128)(2,1)}, bf16[8,128,512]{2,1,0:T(8,128)(2,1)S(1)}, u32[]{:S(2)}, u32[]{:S(2)}) collective-permute-start(bf16[8,128,512]{2,1,0:T(8,128)(2,1)} %param.5), channel_id=1, source_target_pairs={{0,28},{4,0},{8,4},{12,8},{16,12},{20,16},{24,20},{28,24},{1,29},{... | collective-permute-start | bytes 3145736 | tf_op jit(solution)/shard_map/ppermute | solution.py:54
  31.2 17.6 %collective-permute-start.3 = (bf16[8,128,512]{2,1,0:T(8,128)(2,1)S(1)}, bf16[8,128,512]{2,1,0:T(8,128)(2,1)S(1)}, u32[]{:S(2)}, u32[]{:S(2)}) collective-permute-start(bf16[8,128,512]{2,1,0:T(8,128)(2,1)S(1)} %collective-permute-done.1), channel_id=1, source_target_pairs={{0,4},{4,8},{8,12},{12,16},{16,20},{20,24},{24,28},{28,0},{1,5},{5... | collective-permute-start | bytes 3145736 | tf_op jit(solution)/shard_map/ppermute | solution.py:52
  31.9 18.9 %copy-start = (bf16[4,8,1024,128]{3,2,1,0:T(8,128)(2,1)S(1)}, bf16[4,8,1024,128]{3,2,1,0:T(8,128)(2,1)}, u32[]{:S(2)}) copy-start(bf16[4,8,1024,128]{3,2,1,0:T(8,128)(2,1)} %param.6) | copy-start | bytes 25165828
  38.2 22.5 %collective-permute-start.2 = (bf16[8,128,512]{2,1,0:T(8,128)(2,1)S(1)}, bf16[8,128,512]{2,1,0:T(8,128)(2,1)S(1)}, u32[]{:S(2)}, u32[]{:S(2)}) collective-permute-start(bf16[8,128,512]{2,1,0:T(8,128)(2,1)S(1)} %collective-permute-done), channel_id=1, source_target_pairs={{0,28},{4,0},{8,4},{12,8},{16,12},{20,16},{24,20},{28,24},{1,29},{... | collective-permute-start | bytes 3145736 | tf_op jit(solution)/shard_map/ppermute | solution.py:54
  48.8 23.1 %collective-permute-start.5 = (bf16[8,128,512]{2,1,0:T(8,128)(2,1)S(1)}, bf16[8,128,512]{2,1,0:T(8,128)(2,1)S(1)}, u32[]{:S(2)}, u32[]{:S(2)}) collective-permute-start(bf16[8,128,512]{2,1,0:T(8,128)(2,1)S(1)} %collective-permute-done.3), channel_id=1, source_target_pairs={{0,4},{4,8},{8,12},{12,16},{16,20},{20,24},{24,28},{28,0},{1,5},{5... | collective-permute-start | bytes 3145736 | tf_op jit(solution)/shard_map/ppermute | solution.py:52
  60.7 23.4 %collective-permute-start.4 = (bf16[8,128,512]{2,1,0:T(8,128)(2,1)S(1)}, bf16[8,128,512]{2,1,0:T(8,128)(2,1)S(1)}, u32[]{:S(2)}, u32[]{:S(2)}) collective-permute-start(bf16[8,128,512]{2,1,0:T(8,128)(2,1)S(1)} %collective-permute-done.2), channel_id=1, source_target_pairs={{0,28},{4,0},{8,4},{12,8},{16,12},{20,16},{24,20},{28,24},{1,29},{... | collective-permute-start | bytes 3145736 | tf_op jit(solution)/shard_map/ppermute | solution.py:54
  71.9 19.4 %collective-permute-start.6 = (bf16[8,128,512]{2,1,0:T(8,128)(2,1)S(1)}, bf16[8,128,512]{2,1,0:T(8,128)(2,1)S(1)}, u32[]{:S(2)}, u32[]{:S(2)}) collective-permute-start(bf16[8,128,512]{2,1,0:T(8,128)(2,1)S(1)} %collective-permute-done.5), channel_id=1, source_target_pairs={{0,4},{4,8},{8,12},{12,16},{16,20},{20,24},{24,28},{28,0},{1,5},{5... | collective-permute-start | bytes 3145736 | tf_op jit(solution)/shard_map/ppermute | solution.py:52
  117.7 0.7 copy-start.2
  269.4 30.3 %all-to-all-start = ((bf16[8,256,512]{1,2,0:T(8,128)(2,1)}), bf16[8,256,512]{1,2,0:T(8,128)(2,1)S(1)}, u32[]{:S(2)}, u32[]{:S(2)}) async-start(bf16[8,256,512]{1,2,0:T(8,128)(2,1)} %select_select_fusion), calls=%async_computation.1 | async-start | bytes 4194304 | tf_op jit(solution)/shard_map/all_to_all | solution.py:80
Sparse Core Ops, SparseCore 0:
  117.8 147.4 reduce-scatter.1
